TPU v7x, 128 devices: a whole 4x4x4 slice. The times are simulated.
128 devices in a mesh: tm: 4 (over x), feed: 32 (over y, z, core).
Axes of the slice: x: 4, y: 4, z: 4, core: 2. Of those that a mesh axis runs over, the one named last changes fastest.
Arguments:
- voltages: bfloat16 [2048, 98304], P('feed', 'tm'), may hold values from -6 to 6
- gains: bfloat16 [2, 2048, 1024], P(None, 'feed'), may hold values from -4 to 4
- beam_weights: bfloat16 [2, 2048, 2048], replicated, may hold values from -0.09375 to 0.09375
- delay_filter: float32 [1024, 1024], replicated, may hold values from -0.21875 to 0.21875
- channel_lists: int32 [32, 48], replicated, may hold values from -1 to 1023, as said below
- beam_order: int32 [2048], replicated, may hold values from 0 to 2047, each once
Outputs:
- filtered: float32 [4, 2048, 1024], P('tm', 'feed')
Inputs may be any that keep to these rules, and one draw needn't show every extreme that they name: `channel_lists`: each row holds distinct channel numbers in its first places and -1 in the rest; 768 channel numbers are listed in all, none twice; a row lists 0 to 48 channels, and some row lists exactly 48.
All inputs are finite; a program needn't handle non-finite values.
Results may differ from a plain program's by a relative error of at most 0.0021.
Values may be sent and summed in bfloat16 or wider, within the bound.
No kernel may reach another device: no remote copies, remote signals or barrier semaphores. Data moves between devices by JAX's collectives and lax.ppermute only.
A program may use at most 192 MiB of HBM per device.

v0:
```python
import jax
import jax.numpy as jnp
from jax import lax
from jax.sharding import PartitionSpec as P

FFT = 2048
BEAMS = 2048
CHANNELS = 1024
LIVE = 768


def from_behind(block, axis, distance):
    devices = range(lax.axis_size(axis))
    route = [(i - distance, i) for i in devices if i - distance in devices]
    return lax.ppermute(block, axis, route)


def make_window(length):
    places = jnp.arange(4 * length, dtype=jnp.float32)
    centred = (places - 2.0 * length + 0.5) / length
    taper = 0.5 - 0.5 * jnp.cos(2.0 * jnp.pi * (places + 0.5) / (4.0 * length))
    return (jnp.sinc(centred) * taper).reshape(4, length)


def make_table(length):
    sample_rows = jnp.arange(length, dtype=jnp.int32)[:, None]
    channel_cols = jnp.arange(length // 2, dtype=jnp.int32)[None, :]
    phases = (sample_rows * channel_cols % length).astype(jnp.float32)
    angles = 2.0 * jnp.pi * phases / length
    scaling = length ** (-0.5)
    return jnp.concatenate([jnp.cos(angles) * scaling, -jnp.sin(angles) * scaling], axis=1).astype(
        jnp.bfloat16
    )


def filterbank(extended, window, dft_table, frame_count):
    weighted = window[0] * extended[:, 0:frame_count].astype(jnp.float32)
    for tap_index in range(1, 4):
        weighted = weighted + window[tap_index] * extended[
            :, tap_index : tap_index + frame_count
        ].astype(jnp.float32)
    weighted = weighted.astype(jnp.bfloat16)
    rows = weighted.shape[0] * frame_count
    spectra = jnp.dot(
        weighted.reshape(rows, weighted.shape[2]), dft_table, preferred_element_type=jnp.float32
    )
    return spectra.reshape(weighted.shape[0], frame_count, dft_table.shape[1])


def body(voltages, gains, beam_weights, delay_filter, channel_lists, beam_order):
    groups = lax.axis_size("feed")
    inputs_here = voltages.shape[0]
    frames_here = voltages.shape[1] // FFT
    frames = voltages.reshape(inputs_here, frames_here, FFT)
    earlier = from_behind(frames[:, frames_here - 3 :], "tm", 1)
    extended = jnp.concatenate([earlier, frames], axis=1)
    spectra = filterbank(extended, make_window(FFT), make_table(FFT), frames_here)
    flattened = channel_lists.reshape(-1)
    listed = flattened >= 0
    rank_order = jnp.cumsum(listed.astype(jnp.int32)) - 1
    target = jnp.where(listed, rank_order, LIVE)
    slot_ids = jax.ops.segment_sum(jnp.where(listed, flattened, 0), target, num_segments=LIVE + 1)[
        :LIVE
    ]
    slot_count = slot_ids.shape[0] // groups
    present = slot_ids >= 0
    safe_ids = jnp.where(present, slot_ids, 0)
    weight_keep = present.astype(jnp.float32)
    real_part = jnp.take(spectra[:, :, :CHANNELS], safe_ids, axis=2)
    imag_part = jnp.take(spectra[:, :, CHANNELS:], safe_ids, axis=2)
    gain_real = jnp.take(gains[0], safe_ids, axis=1).astype(jnp.float32)[:, None, :]
    gain_imag = jnp.take(gains[1], safe_ids, axis=1).astype(jnp.float32)[:, None, :]
    gained_real = ((real_part * gain_real - imag_part * gain_imag) * weight_keep).astype(
        jnp.bfloat16
    )
    gained_imag = ((real_part * gain_imag + imag_part * gain_real) * weight_keep).astype(
        jnp.bfloat16
    )
    stacked = jnp.stack([gained_real, gained_imag], axis=1)
    stacked = stacked.reshape(inputs_here, 2, frames_here, groups, slot_count)
    outgoing = jnp.transpose(stacked, (3, 0, 1, 4, 2)).reshape(
        groups, inputs_here, 2 * slot_count * frames_here
    )
    received = lax.all_to_all(outgoing, "feed", split_axis=0, concat_axis=1, tiled=True)
    received = received.reshape(groups * inputs_here, 2 * slot_count * frames_here)
    weights = beam_weights.reshape(2 * BEAMS, beam_weights.shape[2])
    product = jnp.dot(weights, received, preferred_element_type=jnp.float32)
    columns = slot_count * frames_here
    beams_real = product[:BEAMS, :columns] - product[BEAMS:, columns:]
    beams_imag = product[:BEAMS, columns:] + product[BEAMS:, :columns]
    powers = (beams_real * beams_real + beams_imag * beams_imag).reshape(
        BEAMS, slot_count, frames_here
    )
    powers = jnp.mean(powers, axis=2)
    ordered = powers[beam_order].reshape(groups, BEAMS // groups, slot_count)
    owned = lax.all_to_all(ordered, "feed", split_axis=0, concat_axis=2, tiled=True)
    owned = owned.reshape(BEAMS // groups, groups * slot_count)
    filter_rows = delay_filter[safe_ids] * weight_keep[:, None]
    filtered = jnp.dot(
        owned, filter_rows, precision=lax.Precision.HIGHEST, preferred_element_type=jnp.float32
    )
    return filtered.reshape(1, BEAMS // groups, CHANNELS)


def solution(mesh):
    placed = (P("feed", "tm"), P(None, "feed", None), P(), P(), P(), P())
    return jax.shard_map(
        body, mesh=mesh, in_specs=placed, out_specs=P("tm", "feed", None), check_vma=False
    )
```

profile of v0, /device:TPU:1, one launch (start us, length us, event | category | flops | bytes accessed | tf_op | source)
XLA Modules:
  0.0 222.3 jit_solution(1583619955177535743)
XLA Ops:
  0.0 5.6 %reshape.123 = bf16[64,12,2048]{2,1,0:T(8,128)(2,1)} reshape(bf16[64,24576]{1,0:T(8,128)(2,1)} %param.10) | data formatting | bytes 6291456 | tf_op jit(solution)/shard_map/reshape | solution.py:54
  5.6 2.2 %slice.96 = bf16[64,3,2048]{2,1,0:T(4,128)(2,1)S(1)} slice(bf16[64,12,2048]{2,1,0:T(8,128)(2,1)} %reshape.123), slice={[0:64], [9:12], [0:2048]} | slice | bytes 1572864 | tf_op jit(solution)/shard_map/slice | solution.py:55
  8.4 4.0 %collective-permute-start = (bf16[64,3,2048]{2,0,1:T(8,128)(2,1)S(1)}, bf16[64,3,2048]{2,0,1:T(8,128)(2,1)S(1)}, u32[]{:S(2)}, u32[]{:S(2)}) collective-permute-start(bf16[64,3,2048]{2,0,1:T(8,128)(2,1)S(1)} %copy.46), channel_id=1, source_target_pairs={{0,32},{32,64},{64,96},{1,33},{33,65},{65,97},{2,34},{34,66},{66,9... | collective-permute-start | bytes 2359304 | tf_op jit(solution)/shard_map/ppermute | solution.py:15
  13.5 11.3 %scatter_custom_fusion = s32[769]{0:T(1024)S(1)} fusion(s32[1536]{0:T(1024)S(1)} %fusion.57, s32[1536]{0:T(1024)S(1)} %compare_select_fusion.1, s32[]{:T(128)} %constant.105.clone.1), kind=kCustom, calls=%fused_computation.103 | custom fusion | flops 1536 | bytes 3080 | tf_op jit(solution)/shard_map/scatter-add | solution.py:62
  25.2 1.9 gather_fusion.3
  27.1 1.9 gather_fusion.5
  29.0 0.9 bitcast_convert_fusion.1
  29.9 34.1 %multiply_convert_fusion = (bf16[2048,1024]{1,0:T(8,128)(2,1)S(1)}, bf16[2048,1024]{1,0:T(8,128)(2,1)S(1)}) fusion(), kind=kLoop, calls=%fused_computation.17 | loop fusion | flops 39845888 | bytes 8388608 | tf_op jit(solution)/shard_map/convert.2
  64.7 5.7 %add_convert_fusion = bf16[64,12,2048]{2,1,0:T(8,128)(2,1)S(1)} fusion(bf16[64,12,2048]{2,1,0:T(8,128)(2,1)S(1)} %copy-done, bf16[64,3,2048]{2,1,0:T(4,128)(2,1)S(1)} %copy.47, f32[2048]{0:T(1024)S(1)} %get-tuple-element.16, f32[2048]{0:T(1024)S(1)} %get-tuple-element.17, f32[2048]{0:T(1024)S(1)} %get-tuple-element.18, f32[2048]{0:T(1024)S(1)} %get-tuple-element.15), kind=kLoop, calls=%fused_computation.21 | loop fusion | flops 33030144 | bytes 7110656 | tf_op jit(solution)/shard_map/convert_element_type | solution.py:42
  70.5 7.4 %fusion.3 = f32[64,12,2048]{2,0,1:T(8,128)S(1)} fusion(bf16[2048,1024]{1,0:T(8,128)(2,1)S(1)} %get-tuple-element.23, bf16[2048,1024]{1,0:T(8,128)(2,1)S(1)} %get-tuple-element.24, bf16[64,12,2048]{2,1,0:T(8,128)(2,1)S(1)} %add_convert_fusion), kind=kOutput, calls=%fused_computation.14 | convolution fusion | flops 6459228160 | bytes 17825792 | tf_op jit(solution)/shard_map/dot_general | solution.py:44
  77.9 2.5 %fusion.62 = (f32[64,12,1024]{2,0,1:T(8,128)S(1)}, f32[64,12,1024]{2,0,1:T(8,128)}) fusion(f32[64,12,2048]{2,0,1:T(8,128)S(1)} %fusion.3), kind=kLoop, calls=%fused_computation.107 | loop fusion | bytes 12582912 | tf_op jit(solution)/shard_map/slice | solution.py:69
  80.3 7.9 %copy.51 = f32[64,12,1024]{0,1,2:T(8,128)} copy(f32[64,12,1024]{2,0,1:T(8,128)} %get-tuple-element.12) | data formatting | bytes 6291456 | tf_op jit(solution)/shard_map/slice | solution.py:70
  88.2 7.3 %gather_fusion.4 = f32[768,64,12]{1,2,0:T(8,128)} fusion(f32[64,12,1024]{0,1,2:T(8,128)} %copy.51, s32[1024]{0:T(1024)S(1)} %pad_clamp_fusion), kind=kCustom, calls=%fused_computation.2.clone | custom fusion | bytes 4721664 | tf_op jit(solution)/shard_map/jit(_take)/gather | solution.py:70
  95.5 6.3 %copy.49 = f32[64,12,1024]{0,1,2:T(8,128)} copy(f32[64,12,1024]{2,0,1:T(8,128)S(1)} %get-tuple-element.11) | data formatting | bytes 6291456 | tf_op jit(solution)/shard_map/slice | solution.py:69
  101.8 7.2 %gather_fusion.2 = f32[768,64,12]{1,2,0:T(8,128)} fusion(f32[64,12,1024]{0,1,2:T(8,128)} %copy.49, s32[1024]{0:T(1024)S(1)} %pad_clamp_fusion), kind=kCustom, calls=%fused_computation.clone | custom fusion | bytes 4721664 | tf_op jit(solution)/shard_map/jit(_take)/gather | solution.py:69
  109.0 8.5 %fusion.11 = (bf16[64,12,768]{0,1,2:T(8,128)(2,1)S(1)}, bf16[64,12,768]{0,1,2:T(8,128)(2,1)S(1)}) fusion(f32[768,64,12]{1,2,0:T(8,128)} %gather_fusion.4, f32[768,64,12]{1,2,0:T(8,128)} %gather_fusion.2, f32[768]{0:T(1024)S(1)} %get-tuple-element.20, f32[64,768]{0,1:T(8,128)S(1)} %copy-done.2, f32[64,768]{0,1:T(8,128)S(1)} %get-tuple-element.21, ...), kind=kLoop, calls=%fused_computation.28 | loop fusion | flops 7077888 | bytes 7474944 | tf_op jit(solution)/shard_map/convert_element_type | solution.py:73
  118.7 1.1 maximum_bitcast_fusion.2
  119.8 3.3 %copy.55 = bf16[32,64,2,24,12]{1,0,4,3,2:T(8,128)(2,1)} copy(bf16[32,64,2,24,12]{1,3,0,4,2:T(8,128)(2,1)S(1)} %maximum_bitcast_fusion.2) | data formatting | bytes 4718592 | tf_op jit(solution)/shard_map/transpose | solution.py:81
  123.0 7.7 %copy.56 = bf16[32,64,576]{2,1,0:T(8,128)(2,1)} copy(bf16[32,64,576]{1,0,2:T(8,128)(2,1)} %bitcast.63) | data formatting | bytes 4718592 | tf_op jit(solution)/shard_map/reshape | solution.py:81
  130.8 9.1 %all-to-all-start = ((bf16[32,64,576]{2,1,0:T(8,128)(2,1)}), bf16[32,64,576]{2,1,0:T(8,128)(2,1)S(1)}, u32[]{:S(2)}, u32[]{:S(2)}) async-start(bf16[32,64,576]{2,1,0:T(8,128)(2,1)} %copy.56), calls=%async_computation | async-start | bytes 5242880 | tf_op jit(solution)/shard_map/all_to_all | solution.py:84
  139.9 33.9 %all-to-all-done = bf16[32,64,576]{2,1,0:T(8,128)(2,1)S(1)} async-done(((bf16[32,64,576]{2,1,0:T(8,128)(2,1)}), bf16[32,64,576]{2,1,0:T(8,128)(2,1)S(1)}, u32[]{:S(2)}, u32[]{:S(2)}) %all-to-all-start) | async-done | bytes 2359328 | tf_op jit(solution)/shard_map/all_to_all | solution.py:84
  173.8 1.5 copy-done.1
  175.3 15.3 %convolution_bitcast_fusion = f32[4096,576]{0,1:T(8,128)S(1)} fusion(bf16[2048,576]{1,0:T(8,128)(2,1)} %bitcast.69, bf16[4096,2048]{1,0:T(8,128)(2,1)} %bitcast.72), kind=kOutput, calls=%fused_computation.23 | convolution fusion | flops 9663676416 | bytes 28573696 | tf_op jit(solution)/shard_map/dot_general | solution.py:87
  190.5 2.4 %fusion.21 = f32[2048,288]{0,1:T(8,128)} fusion(f32[4096,576]{0,1:T(8,128)S(1)} %convolution_bitcast_fusion), kind=kLoop, calls=%fused_computation.45 | loop fusion | flops 2949120 | bytes 11796480 | tf_op jit(solution)/shard_map/add | solution.py:91
  193.0 2.4 %reshape.129 = f32[2048,24,12]{0,2,1:T(8,128)S(1)} reshape(f32[2048,288]{0,1:T(8,128)} %fusion.21) | data formatting | bytes 4718592 | tf_op jit(solution)/shard_map/reshape | solution.py:91
  196.4 5.5 %gather_fusion = f32[2048,24]{1,0:T(8,128)S(1)} fusion(f32[2048,24]{1,0:T(8,128)S(1)} %copy.57, s32[2048]{0:T(1024)S(1)} %fusion.56), kind=kCustom, calls=%fused_computation.4 | custom fusion | bytes 401408 | tf_op jit(solution)/shard_map/gather | solution.py:95
  203.1 4.4 %all-to-all-start.1 = ((f32[32,1,1536]{2,1,0:T(1,128)}), f32[32,1,1536]{2,1,0:T(1,128)S(1)}, u32[]{:S(2)}, u32[]{:S(2)}) async-start(f32[32,1,1536]{2,1,0:T(1,128)} %reshape.209), calls=%async_computation.1 | async-start | bytes 393216 | tf_op jit(solution)/shard_map/all_to_all | solution.py:96
  207.5 6.1 %gather_fusion.1 = f32[768,1024]{1,0:T(8,128)S(1)} fusion(f32[1024,1024]{1,0:T(8,128)} %param.13, s32[1024]{0:T(1024)S(1)} %pad_clamp_fusion), kind=kCustom, calls=%fused_computation.5 | custom fusion | bytes 6294528 | tf_op jit(solution)/shard_map/gather | solution.py:98
  213.6 2.3 %all-to-all-done.1 = f32[32,1,1536]{2,1,0:T(1,128)S(1)} async-done(((f32[32,1,1536]{2,1,0:T(1,128)}), f32[32,1,1536]{2,1,0:T(1,128)S(1)}, u32[]{:S(2)}, u32[]{:S(2)}) %all-to-all-start.1) | async-done | bytes 196640 | tf_op jit(solution)/shard_map/all_to_all | solution.py:96
  216.5 1.8 reduce.4
  218.3 1.0 reshape.210
  219.4 2.9 %fusion.24 = f32[1,64,1024]{2,1,0:T(8,128)} fusion(f32[64,768]{0,1:T(8,128)S(1)} %bitcast.70, f32[768,1024]{1,0:T(8,128)S(1)} %gather_fusion.1, f32[768]{0:T(1024)S(1)} %get-tuple-element.20), kind=kOutput, calls=%fused_computation.49 | convolution fusion | flops 604766208 | bytes 3607552 | tf_op jit(solution)/shard_map/dot_general | solution.py:99
  (42 shorter events, 6.7 us)
Async XLA Ops:
  0.0 12.6 %copy-start.4 = (s32[32,48]{1,0:T(8,128)S(1)}, s32[32,48]{1,0:T(8,128)}, u32[]{:S(2)}) copy-start(s32[32,48]{1,0:T(8,128)} %param.14) | copy-start | bytes 18436
  0.0 24.8 %copy-start.3 = (bf16[2,64,1024]{2,1,0:T(8,128)(2,1)S(1)}, bf16[2,64,1024]{2,1,0:T(8,128)(2,1)}, u32[]{:S(2)}) copy-start(bf16[2,64,1024]{2,1,0:T(8,128)(2,1)} %param.11) | copy-start | bytes 786436
  8.4 55.6 %collective-permute-start = (bf16[64,3,2048]{2,0,1:T(8,128)(2,1)S(1)}, bf16[64,3,2048]{2,0,1:T(8,128)(2,1)S(1)}, u32[]{:S(2)}, u32[]{:S(2)}) collective-permute-start(bf16[64,3,2048]{2,0,1:T(8,128)(2,1)S(1)} %copy.46), channel_id=1, source_target_pairs={{0,32},{32,64},{64,96},{1,33},{33,65},{65,97},{2,34},{34,66},{66,9... | collective-permute-start | bytes 2359304 | tf_op jit(solution)/shard_map/ppermute | solution.py:15
  29.0 35.7 %copy-start = (bf16[64,12,2048]{2,1,0:T(8,128)(2,1)S(1)}, bf16[64,12,2048]{2,1,0:T(8,128)(2,1)}, u32[]{:S(2)}) copy-start(bf16[64,12,2048]{2,1,0:T(8,128)(2,1)} %reshape.123) | copy-start | bytes 9437188
  101.8 7.2 %copy-start.2 = (f32[64,768]{0,1:T(8,128)S(1)}, f32[64,768]{0,1:T(8,128)}, u32[]{:S(2)}) copy-start(f32[64,768]{0,1:T(8,128)} %get-tuple-element.22) | copy-start | bytes 589828
  123.0 16.8 %copy-start.5 = (s32[2048]{0:T(1024)S(1)}, s32[2048]{0:T(1024)}, u32[]{:S(2)}) copy-start(s32[2048]{0:T(1024)} %param.15) | copy-start | bytes 24580
  130.8 43.0 %all-to-all-start = ((bf16[32,64,576]{2,1,0:T(8,128)(2,1)}), bf16[32,64,576]{2,1,0:T(8,128)(2,1)S(1)}, u32[]{:S(2)}, u32[]{:S(2)}) async-start(bf16[32,64,576]{2,1,0:T(8,128)(2,1)} %copy.56), calls=%async_computation | async-start | bytes 5242880 | tf_op jit(solution)/shard_map/all_to_all | solution.py:84
  173.8 1.5 copy-start.1
  203.1 12.8 %all-to-all-start.1 = ((f32[32,1,1536]{2,1,0:T(1,128)}), f32[32,1,1536]{2,1,0:T(1,128)S(1)}, u32[]{:S(2)}, u32[]{:S(2)}) async-start(f32[32,1,1536]{2,1,0:T(1,128)} %reshape.209), calls=%async_computation.1 | async-start | bytes 393216 | tf_op jit(solution)/shard_map/all_to_all | solution.py:96
where the time goes:
time: 223 us; the launch traced here: 222 us
  local copies, waits for them, and re-layouts  75.7 us (34%)
  other arithmetic  67.2 us (30%)
  waiting for transfers between devices  36.2 us (16%)
  matrix products  25.5 us (11%)
  starting transfers between devices  17.5 us (8%)
    another operation x3, other arithmetic  34.4 us
    all_to_all x1, waiting for transfers between devices, body(): lax.all_to_all(outgoing, 'feed', split_axis=0, concat_axis=1, tiled=True)  33.9 us
    dot_general x1, matrix products, body(): product = jnp.dot(weights, received, preferred_element_type=jnp.float32)  15.3 us
    scatter-add x1, other arithmetic, body(): jax.ops.segment_sum(jnp.where(listed, flattened, 0), target, num_segments...  11.3 us
    all_to_all x1, starting transfers between devices, body(): lax.all_to_all(outgoing, 'feed', split_axis=0, concat_axis=1, tiled=True)  9.07 us
    slice x2, local copies, waits for them, and re-layouts, body(): real_part = jnp.take(spectra[:, :, :CHANNELS], safe_ids, axis=2)  8.77 us
    convert_element_type x1, other arithmetic, body(): ((real_part * gain_real - imag_part * gain_imag) * weight_keep).astype(jn...  8.51 us
    slice x1, local copies, waits for them, and re-layouts, body(): imag_part = jnp.take(spectra[:, :, CHANNELS:], safe_ids, axis=2)  7.86 us
  transfers between devices with their start and end apart: 3, of which 2 were waited for; matrix products, arithmetic and copies ran while one was open for 26% of the time, Pallas kernels for 0%

commit v1 on v0

v1 whole, which is shorter than its diff:
```python
import functools

import jax
import jax.numpy as jnp
import numpy as np
from jax import lax
from jax.experimental import pallas as pl
from jax.experimental.pallas import tpu as pltpu
from jax.sharding import PartitionSpec as P

FFT = 2048
BEAMS = 2048
CHANNELS = 1024
LIVE = 768
FR = 12
LATE = 4
NT = (((1,), (1,)), ((), ()))
TN = (((0,), (0,)), ((), ()))
F32 = jnp.float32
BF16 = jnp.bfloat16


def make_window(length):
    places = np.arange(4 * length, dtype=np.float64)
    centred = (places - 2.0 * length + 0.5) / length
    taper = 0.5 - 0.5 * np.cos(2.0 * np.pi * (places + 0.5) / (4.0 * length))
    return (np.sinc(centred) * taper).reshape(4, length).astype(np.float32)


def cos_sin(phase):
    quarter = lax.shift_right_logical(phase + 256, 9)
    x = (phase - quarter * 512).astype(F32) * np.float32(np.pi / 1024)
    y = x * x
    s = x * (1.0 + y * (-1.0 / 6 + y * (1.0 / 120 + y * (-1.0 / 5040 + y * (1.0 / 362880)))))
    c = 1.0 + y * (
        -0.5 + y * (1.0 / 24 + y * (-1.0 / 720 + y * (1.0 / 40320 + y * (-1.0 / 3628800))))
    )
    odd = (quarter & 1) == 1
    cos = jnp.where(odd, s, c)
    sin = jnp.where(odd, c, s)
    cos = jnp.where(((quarter + 1) & 2) == 2, -cos, cos)
    sin = jnp.where((quarter & 2) == 2, -sin, sin)
    return cos, sin


def slots_of(lists):
    groups, places = lists.shape
    listed = (lists >= 0).astype(F32)
    counts = jnp.sum(listed, axis=1, keepdims=True)
    above = lax.broadcasted_iota(jnp.int32, (groups, groups), 0)
    here = lax.broadcasted_iota(jnp.int32, (groups, groups), 1)
    wide = jnp.broadcast_to(counts, (groups, groups))
    first = jnp.sum(jnp.where(above < here, wide, 0.0), axis=0, keepdims=True)
    count = jnp.sum(jnp.where(above == here, wide, 0.0), axis=0, keepdims=True)
    slot = lax.broadcasted_iota(jnp.int32, (LIVE, groups), 0).astype(F32)
    inside = (slot >= first) & (slot < first + count)
    pick = jnp.where(inside, 1.0, 0.0)
    place = jnp.sum(jnp.where(inside, slot - first, 0.0), axis=1, keepdims=True)
    known = jnp.maximum(lists, 0)
    high = (known >> 5).astype(F32).astype(BF16)
    low = (known & 31).astype(F32).astype(BF16)
    pick = pick.astype(BF16)
    rows = 32.0 * jnp.dot(pick, high, preferred_element_type=F32) + jnp.dot(
        pick, low, preferred_element_type=F32
    )
    across = lax.broadcasted_iota(jnp.int32, (LIVE, places), 1).astype(F32)
    return jnp.sum(jnp.where(across == place, rows, 0.0), axis=1, keepdims=True)


def fir(read, window_ref, weighted_ref, count, inputs):
    def tile(step, carry):
        lane = pl.multiple_of(step * 128, 128)
        taps = [window_ref[pl.ds(t, 1), pl.ds(lane, 128)] for t in range(4)]
        for row in range(0, inputs, 16):
            frames = [read(f, row, lane).astype(F32) for f in range(count + 3)]
            for k in range(count):
                total = taps[0] * frames[k]
                for t in range(1, 4):
                    total = total + taps[t] * frames[k + t]
                weighted_ref[pl.ds(k * inputs + row, 16), pl.ds(lane, 128)] = total.astype(BF16)
        return carry

    lax.fori_loop(0, FFT // 128, tile, 0)


def spectra_and_gains(table_ref, weighted_ref, gain_ref, out_ref, groups, width):
    half = groups // 2
    rows = 2 * LIVE // 2
    share = LIVE // groups

    def part(step, carry):
        block = step % 2
        lane = pl.multiple_of((step // 2) * 256, 256)
        product = lax.dot_general(
            table_ref[pl.ds(pl.multiple_of(block * rows, rows), rows), :],
            weighted_ref[pl.ds(lane, 256), :],
            NT,
            preferred_element_type=F32,
        )
        for g in range(half):
            here = block * half + g
            at = pl.multiple_of(here * share, share)
            real_gain = gain_ref[pl.ds(at, share), 0:128]
            imag_gain = gain_ref[pl.ds(at, share), 128:256]
            for piece in range(2):
                cut = slice(piece * 128, piece * 128 + 128)
                real = product[g * 2 * share : g * 2 * share + share, cut]
                imag = product[g * 2 * share + share : (g + 1) * 2 * share, cut]
                both = jnp.concatenate(
                    [
                        real * real_gain - imag * imag_gain,
                        real * imag_gain + imag * real_gain,
                    ],
                    axis=0,
                )
                out_ref[here, :, pl.ds(lane + piece * 128, 128)] = both.astype(BF16)
        return carry

    lax.fori_loop(0, 2 * (width // 256), part, 0)


def early_kernel(
    lists_ref, gains_ref, window_ref, volts_ref,
    out_ref, table_ref, gain_ref, pick_ref, channel_ref, weighted_ref,
):
    groups = lists_ref.shape[0]
    inputs = volts_ref.shape[0]
    share = LIVE // groups
    channel_ref[...] = jnp.broadcast_to(slots_of(lists_ref[...]), (LIVE, 128)).astype(jnp.int32)

    def table_rows(g, carry):
        at = pl.multiple_of(g * share, share)
        channel = channel_ref[pl.ds(at, share), :]
        lane = lax.broadcasted_iota(jnp.int32, (share, 128), 1)
        cos, sin = cos_sin((channel * lane) & (FFT - 1))
        scale = np.float32(FFT ** (-0.5))
        real, imag = cos * scale, -sin * scale
        turn_cos, turn_sin = cos_sin((channel * 128) & (FFT - 1))
        for j in range(FFT // 128):
            both = jnp.concatenate([real, imag], axis=0).astype(BF16)
            table_ref[pl.ds(pl.multiple_of(g * 2 * share, 2 * share), 2 * share), j * 128 : (j + 1) * 128] = both
            real, imag = real * turn_cos + imag * turn_sin, imag * turn_cos - real * turn_sin
        for j in range(CHANNELS // 128):
            pick_ref[pl.ds(at, share), j * 128 : (j + 1) * 128] = jnp.where(
                channel == lane + j * 128, 1.0, 0.0
            ).astype(BF16)
        return carry

    lax.fori_loop(0, groups, table_rows, 0)
    gain = lax.dot_general(pick_ref[...], gains_ref[...], NT, preferred_element_type=F32)
    turned = pltpu.roll(gain, 64, 1)
    low = lax.broadcasted_iota(jnp.int32, gain.shape, 1) < 64
    gain_ref[:, 0:128] = jnp.where(low, gain, turned)
    gain_ref[:, 128:256] = jnp.where(low, turned, gain)

    def read(f, row, lane):
        return volts_ref[pl.ds(row, 16), pl.ds(lane + (f + LATE - 3) * FFT, 128)]

    count = FR - LATE
    fir(read, window_ref, weighted_ref, count, inputs)
    spectra_and_gains(table_ref, weighted_ref, gain_ref, out_ref, groups, count * inputs)


def late_kernel(table_ref, gain_ref, window_ref, before_ref, volts_ref, out_ref, weighted_ref):
    groups = out_ref.shape[0]
    inputs = volts_ref.shape[0]

    def read(f, row, lane):
        if f < 3:
            return before_ref[pl.ds(row, 16), pl.ds(lane + f * FFT, 128)]
        return volts_ref[pl.ds(row, 16), pl.ds(lane + (f - 3) * FFT, 128)]

    fir(read, window_ref, weighted_ref, LATE, inputs)
    spectra_and_gains(table_ref, weighted_ref, gain_ref, out_ref, groups, LATE * inputs)


def arrange(received_ref, spread_ref):
    groups, rows, width = received_ref.shape
    low = lax.broadcasted_iota(jnp.int32, (rows, 128), 1) < 64
    for pair in range(groups // 2):
        for two in range(width // 128):
            cut = slice(two * 128, two * 128 + 128)
            first = received_ref[2 * pair, :, cut].astype(F32)
            second = received_ref[2 * pair + 1, :, cut].astype(F32)
            one = jnp.where(low, first, pltpu.roll(second, 64, 1))
            other = jnp.where(low, pltpu.roll(first, 64, 1), second)
            at = slice(pair * 128, pair * 128 + 128)
            spread_ref[2 * two * rows : (2 * two + 1) * rows, at] = one.astype(BF16)
            spread_ref[(2 * two + 1) * rows : (2 * two + 2) * rows, at] = other.astype(BF16)


def beam_powers(spread_ref, weights_ref, rows):
    by_real = lax.dot_general(spread_ref[...], weights_ref[0], NT, preferred_element_type=F32)
    by_imag = lax.dot_general(spread_ref[...], weights_ref[1], NT, preferred_element_type=F32)
    half = rows // 2
    total = None
    for k in range(spread_ref.shape[0] // rows):
        top, middle, end = k * rows, k * rows + half, (k + 1) * rows
        real = by_real[top:middle] - by_imag[middle:end]
        imag = by_real[middle:end] + by_imag[top:middle]
        power = real * real + imag * imag
        total = power if total is None else total + power
    return total


def first_beams_kernel(received_ref, weights_ref, out_ref, spread_ref):
    @pl.when(pl.program_id(0) == 0)
    def _():
        arrange(received_ref, spread_ref)

    out_ref[...] = beam_powers(spread_ref, weights_ref, received_ref.shape[1])


def last_beams_kernel(
    received_ref, weights_ref, partial_ref, order_ref, out_ref, spread_ref, powers_ref
):
    step = pl.program_id(0)
    tiles = powers_ref.shape[0]
    per_step = out_ref.shape[0] // 2

    @pl.when(step == 0)
    def _():
        arrange(received_ref, spread_ref)

    total = partial_ref[...] + beam_powers(spread_ref, weights_ref, received_ref.shape[1])
    total = total * np.float32(1.0 / FR)
    here = total.shape[1] // 128
    for j in range(here):
        powers_ref[step * here + j] = total[:, j * 128 : (j + 1) * 128]

    @pl.when(step == pl.num_programs(0) - 1)
    def _():
        rows = powers_ref.shape[1]
        low = lax.broadcasted_iota(jnp.int32, (rows, 128), 1) < 64

        def move(tile, carry):
            order = jnp.broadcast_to(order_ref[pl.ds(tile, 1), :], (rows, 128))
            lane = order & 127
            source = order >> 7
            moved = jnp.zeros((rows, 128), F32)
            for j in range(tiles):
                moved = jnp.where(
                    source == j,
                    jnp.take_along_axis(powers_ref[j], lane, axis=1),
                    moved,
                )
            high = moved.astype(BF16).astype(F32)
            rest = moved - high
            out_ref[2 * tile] = jnp.where(low, high, pltpu.roll(rest, 64, 1)).astype(BF16)
            out_ref[2 * tile + 1] = jnp.where(low, pltpu.roll(high, 64, 1), rest).astype(BF16)
            return carry

        lax.fori_loop(0, tiles, move, 0)


def filter_rows_kernel(pick_ref, filter_ref, high_ref, low_ref):
    whole = filter_ref[...]
    high = whole.astype(BF16)
    low = (whole - high.astype(F32)).astype(BF16)
    high_ref[...] = jnp.dot(pick_ref[...], high, preferred_element_type=F32).astype(BF16)
    low_ref[...] = jnp.dot(pick_ref[...], low, preferred_element_type=F32).astype(BF16)


def filter_kernel(powers_ref, high_ref, low_ref, out_ref):
    powers = powers_ref[...]
    both = lax.dot_general(powers, high_ref[...], TN, preferred_element_type=F32)
    rest = lax.dot_general(powers, low_ref[...], TN, preferred_element_type=F32)
    half = out_ref.shape[0]
    out_ref[...] = (both[half:] + rest[:half]) + both[:half]


def cost(flops, data=0):
    return pl.CostEstimate(flops=int(flops), bytes_accessed=int(data), transcendentals=0)


def params(limit=None, **more):
    return pltpu.CompilerParams(vmem_limit_bytes=limit, **more)


VM = pl.BlockSpec(memory_space=pltpu.VMEM)


def body(voltages, gains, beam_weights, delay_filter, channel_lists, beam_order):
    groups = lax.axis_size("feed")
    steps = lax.axis_size("tm")
    inputs = voltages.shape[0]
    share = LIVE // groups
    mine = BEAMS // groups
    window = jnp.asarray(make_window(FFT))
    before = lax.ppermute(
        voltages[:, (FR - 3) * FFT :], "tm", [(i, i + 1) for i in range(steps - 1)]
    )
    early = (FR - LATE) * inputs
    late = LATE * inputs
    mib = 1 << 20
    spectra, table, gain, pick = pl.pallas_call(
        early_kernel,
        out_shape=(
            jax.ShapeDtypeStruct((groups, 2 * share, early), BF16),
            jax.ShapeDtypeStruct((2 * LIVE, FFT), BF16),
            jax.ShapeDtypeStruct((LIVE, 256), F32),
            jax.ShapeDtypeStruct((LIVE, CHANNELS), BF16),
        ),
        in_specs=[VM] * 4,
        out_specs=(VM,) * 4,
        scratch_shapes=[pltpu.VMEM((LIVE, 128), jnp.int32), pltpu.VMEM((early, FFT), BF16)],
        compiler_params=params(40 * mib),
        cost_estimate=cost(2 * 2 * LIVE * FFT * early),
        name="early",
    )(channel_lists, gains.reshape(2 * inputs, CHANNELS), window, voltages)
    first = lax.all_to_all(spectra, "feed", split_axis=0, concat_axis=0, tiled=True)
    spectra = pl.pallas_call(
        late_kernel,
        out_shape=jax.ShapeDtypeStruct((groups, 2 * share, late), BF16),
        grid=(1,),
        in_specs=[
            VM, VM, VM, VM,
            pl.BlockSpec((inputs, LATE * FFT), lambda i: (0, 0)),
        ],
        out_specs=VM,
        scratch_shapes=[pltpu.VMEM((late, FFT), BF16)],
        compiler_params=params(40 * mib),
        cost_estimate=cost(2 * 2 * LIVE * FFT * late),
        name="late",
    )(table, gain, window, before, voltages)
    filter_high, filter_low = pl.pallas_call(
        filter_rows_kernel,
        out_shape=(jax.ShapeDtypeStruct((LIVE, CHANNELS), BF16),) * 2,
        in_specs=[VM] * 2,
        out_specs=(VM,) * 2,
        compiler_params=params(40 * mib),
        cost_estimate=cost(4 * LIVE * CHANNELS * CHANNELS),
        name="filter_rows",
    )(pick, delay_filter)
    second = lax.all_to_all(spectra, "feed", split_axis=0, concat_axis=0, tiled=True)
    span = 256
    partial = pl.pallas_call(
        first_beams_kernel,
        out_shape=jax.ShapeDtypeStruct((share, BEAMS), F32),
        grid=(BEAMS // span,),
        in_specs=[VM, pl.BlockSpec((2, span, groups * inputs), lambda i: (0, i, 0))],
        out_specs=pl.BlockSpec((share, span), lambda i: (0, i)),
        scratch_shapes=[pltpu.VMEM((2 * share * (FR - LATE), groups * inputs), BF16)],
        compiler_params=params(40 * mib),
        cost_estimate=cost(2 * 2 * BEAMS * groups * inputs * 2 * share * (FR - LATE)),
        name="first_beams",
    )(first, beam_weights)
    powers = pl.pallas_call(
        last_beams_kernel,
        out_shape=jax.ShapeDtypeStruct((groups, share, 2 * mine), BF16),
        grid=(BEAMS // span,),
        in_specs=[
            VM,
            pl.BlockSpec((2, span, groups * inputs), lambda i: (0, i, 0)),
            pl.BlockSpec((share, span), lambda i: (0, i)),
            VM,
        ],
        out_specs=pl.BlockSpec((groups, share, 2 * mine), lambda i: (0, 0, 0)),
        scratch_shapes=[
            pltpu.VMEM((2 * share * LATE, groups * inputs), BF16),
            pltpu.VMEM((BEAMS // 128, share, 128), F32),
        ],
        compiler_params=params(40 * mib),
        cost_estimate=cost(2 * 2 * BEAMS * groups * inputs * 2 * share * LATE),
        name="last_beams",
    )(second, beam_weights, partial, beam_order.reshape(BEAMS // 128, 128))
    owned = lax.all_to_all(powers, "feed", split_axis=0, concat_axis=0, tiled=True)
    filtered = pl.pallas_call(
        filter_kernel,
        out_shape=jax.ShapeDtypeStruct((mine, CHANNELS), F32),
        in_specs=[VM] * 3,
        out_specs=VM,
        compiler_params=params(40 * mib),
        cost_estimate=cost(4 * LIVE * CHANNELS * 2 * mine),
        name="filter",
    )(owned.reshape(LIVE, 2 * mine), filter_high, filter_low)
    return filtered.reshape(1, mine, CHANNELS)


def solution(mesh):
    placed = (P("feed", "tm"), P(None, "feed", None), P(), P(), P(), P())
    return jax.shard_map(
        body, mesh=mesh, in_specs=placed, out_specs=P("tm", "feed", None), check_vma=False
    )
```

time: 223 us -> 111 us (0.50)
  other arithmetic: 67.2 us -> 0 us
  local copies, waits for them, and re-layouts: 75.7 us -> 17.5 us
  Pallas kernels: 0 us -> 45.8 us
  matrix products: 25.5 us -> 0 us
  waiting for transfers between devices: 36.2 us -> 19 us
  starting transfers between devices: 17.5 us -> 27.5 us
    pallas_call x0 -> x6, Pallas kernels: none -> 45.8 us  [the longest x1 15.3 us: body(): pl.pallas_call(last_beams_kernel, out_shape=jax.ShapeDtypeStruct((groups,...]
    another operation x3 -> x0, other arithmetic: 34.4 us -> none
    all_to_all x2 -> x3, waiting for transfers between devices: 36.1 us -> 2.49 us  [the longest x1 1.28 us: body(): lax.all_to_all(powers, 'feed', split_axis=0, concat_axis=0, tiled=True)]
    gather x6 -> x0, local copies, waits for them, and re-layouts: 29.8 us -> none  [the longest x1 7.28 us: body(): imag_part = jnp.take(spectra[:, :, CHANNELS:], safe_ids, axis=2)]
    dot_general x3 -> x0, matrix products: 25.5 us -> none  [the longest x1 15.3 us: body(): product = jnp.dot(weights, received, preferred_element_type=jnp.float32)]
    slice x8 -> x1, local copies, waits for them, and re-layouts: 19.5 us -> 0.05 us  [body(): voltages[:, (FR - 3) * FFT:]]
    ppermute x1, waiting for transfers between devices: 0.01 us -> 16.5 us  [body(): lax.ppermute(voltages[:, (FR - 3) * FFT:], 'tm', [(i, i + 1) for i in ran...]
    reshape x5 -> x0, local copies, waits for them, and re-layouts: 16.1 us -> none  [the longest x1 7.73 us: body(): jnp.transpose(stacked, (3, 0, 1, 4, 2))]
  transfers between devices with their start and end apart: 3 -> 4, of which waited for: 2 -> 3; matrix products, arithmetic and copies ran while one was open for 26% -> 0% of each run, Pallas kernels for 0% -> 18%
where the time goes in v1:
time: 111 us; the launch traced here: 110 us
  Pallas kernels  45.8 us (41%)
  starting transfers between devices  27.5 us (25%)
  waiting for transfers between devices  19 us (17%)
  local copies, waits for them, and re-layouts  17.5 us (16%)
    all_to_all x2, starting transfers between devices, body(): lax.all_to_all(spectra, 'feed', split_axis=0, concat_axis=0, tiled=True)  18 us
    unnamed x32, local copies, waits for them, and re-layouts  17.5 us
    ppermute x1, waiting for transfers between devices, body(): lax.ppermute(voltages[:, (FR - 3) * FFT:], 'tm', [(i, i + 1) for i in ran...  16.5 us
    pallas_call x1, Pallas kernels, body(): pl.pallas_call(last_beams_kernel, out_shape=jax.ShapeDtypeStruct((groups,...  15.3 us
    pallas_call x1, Pallas kernels, body(): pl.pallas_call(first_beams_kernel, out_shape=jax.ShapeDtypeStruct((share,...  13 us
    pallas_call x1, Pallas kernels, body(): pl.pallas_call(early_kernel, out_shape=(jax.ShapeDtypeStruct((groups, 2 *...  9.82 us
    all_to_all x1, starting transfers between devices, body(): lax.all_to_all(powers, 'feed', split_axis=0, concat_axis=0, tiled=True)  6.2 us
    pallas_call x1, Pallas kernels, body(): pl.pallas_call(filter_rows_kernel, out_shape=(jax.ShapeDtypeStruct((LIVE,...  3.42 us
  transfers between devices with their start and end apart: 4, of which 3 were waited for; matrix products, arithmetic and copies ran while one was open for 0% of the time, Pallas kernels for 18%

profile of v1, /device:TPU:1, one launch (start us, length us, event | category | flops | bytes accessed | tf_op | source)
XLA Modules:
  0.0 110.0 jit_solution(3864602623548884786)
XLA Ops:
  0.0 1.9 %copy-done.2 = bf16[64,24576]{1,0:T(8,128)(2,1)S(1)} copy-done((bf16[64,24576]{1,0:T(8,128)(2,1)S(1)}, bf16[64,24576]{1,0:T(8,128)(2,1)}, u32[]{:S(2)}) %copy-start.2) | copy-done | bytes 3145752
  1.9 0.8 copy-done.8
  2.7 0.9 copy-done.12
  3.6 0.7 copy-done.13
  4.3 9.8 %early.1 = (bf16[32,48,512]{2,1,0:T(8,128)(2,1)S(1)}, bf16[1536,2048]{1,0:T(8,128)(2,1)S(1)}, f32[768,256]{1,0:T(8,128)S(1)}, bf16[768,1024]{1,0:T(8,128)(2,1)S(1)}) custom-call(s32[32,48]{1,0:T(8,128)S(1)} %copy-done.13, bf16[128,1024]{1,0:T(8,128)(2,1)S(1)} %bitcast.6, f32[4,2048]{1,0:T(4,128)S(1)} %copy-done.8, bf16[64,24576]{1,0:T(8,128)(2,1)S(1)} %copy-done.2), custom_call_target="tpu_custom_call" | custom-call | flops 3221225472 | tf_op jit(solution)/shard_map/early/pallas_call | solution.py:296
  14.1 0.0 copy-start
  14.2 2.7 %copy-done = bf16[1536,2048]{1,0:T(8,128)(2,1)} copy-done((bf16[1536,2048]{1,0:T(8,128)(2,1)}, bf16[1536,2048]{1,0:T(8,128)(2,1)S(1)}, u32[]{:S(2)}) %copy-start) | copy-done | bytes 6291480
  16.8 1.2 %copy-done.5 = bf16[32,48,512]{2,1,0:T(8,128)(2,1)} copy-done((bf16[32,48,512]{2,1,0:T(8,128)(2,1)}, bf16[32,48,512]{2,1,0:T(8,128)(2,1)S(1)}, u32[]{:S(2)}) %copy-start.5) | copy-done | bytes 1572888
  18.0 0.9 copy-done.6
  18.9 1.1 %copy-done.14 = bf16[768,1024]{1,0:T(8,128)(2,1)} copy-done((bf16[768,1024]{1,0:T(8,128)(2,1)}, bf16[768,1024]{1,0:T(8,128)(2,1)S(1)}, u32[]{:S(2)}) %copy-start.14) | copy-done | bytes 1572888
  20.1 9.9 %all-to-all-start.1 = ((bf16[32,48,512]{2,1,0:T(8,128)(2,1)}), bf16[32,48,512]{2,1,0:T(8,128)(2,1)}, u32[]{:S(2)}, u32[]{:S(2)}) async-start(bf16[32,48,512]{2,1,0:T(8,128)(2,1)} %copy-done.5), calls=%async_computation.1 | async-start | bytes 3145728 | tf_op jit(solution)/shard_map/all_to_all | solution.py:311
  30.0 0.0 copy-start.9
  30.0 0.1 slice.3
  30.1 3.3 %collective-permute-start = (bf16[64,6144]{1,0:T(8,128)(2,1)S(1)}, bf16[64,6144]{1,0:T(8,128)(2,1)S(1)}, u32[]{:S(2)}, u32[]{:S(2)}) collective-permute-start(bf16[64,6144]{1,0:T(8,128)(2,1)S(1)} %slice.3), channel_id=1, source_target_pairs={{0,32},{32,64},{64,96},{1,33},{33,65},{65,97},{2,34},{34,66},{66,9... | collective-permute-start | bytes 2359304 | tf_op jit(solution)/shard_map/ppermute | solution.py:290
  33.4 16.5 %collective-permute-done.before_ref = bf16[64,6144]{1,0:T(8,128)(2,1)S(1)} collective-permute-done((bf16[64,6144]{1,0:T(8,128)(2,1)S(1)}, bf16[64,6144]{1,0:T(8,128)(2,1)S(1)}, u32[]{:S(2)}, u32[]{:S(2)}) %collective-permute-start) | collective-permute-done | bytes 786464 | tf_op jit(solution)/shard_map/ppermute | solution.py:290
  49.9 2.8 %copy-done.1 = bf16[1536,2048]{1,0:T(8,128)(2,1)S(1)} copy-done((bf16[1536,2048]{1,0:T(8,128)(2,1)S(1)}, bf16[1536,2048]{1,0:T(8,128)(2,1)}, u32[]{:S(2)}) %copy-start.1) | copy-done | bytes 6291480
  52.7 2.9 %late.1 = bf16[32,48,256]{2,1,0:T(8,128)(2,1)S(1)} custom-call(bf16[1536,2048]{1,0:T(8,128)(2,1)S(1)} %copy-done.1, f32[768,256]{1,0:T(8,128)S(1)} %copy-done.7, f32[4,2048]{1,0:T(4,128)S(1)} %copy-done.9, bf16[64,6144]{1,0:T(8,128)(2,1)S(1)} %collective-permute-done.before_ref, bf16[64,24576]{1,0:T(8,128)(2,1)S(1)} %copy-done.3), custom_call_target="tpu_custom_call" | custom-call | flops 1610612736 | tf_op jit(solution)/shard_map/late/pallas_call | solution.py:312
  55.6 0.0 copy-start.4
  55.6 0.9 copy-done.4
  56.5 0.0 all-to-all-done.1.received_ref
  56.5 8.2 %all-to-all-start = ((bf16[32,48,256]{2,1,0:T(8,128)(2,1)}), bf16[32,48,256]{2,1,0:T(8,128)(2,1)S(1)}, u32[]{:S(2)}, u32[]{:S(2)}) async-start(bf16[32,48,256]{2,1,0:T(8,128)(2,1)} %copy-done.4), calls=%async_computation | async-start | bytes 1572864 | tf_op jit(solution)/shard_map/all_to_all | solution.py:335
  64.6 0.0 copy-start.10
  64.7 13.0 %first_beams.1.partial_ref = f32[24,2048]{1,0:T(8,128)S(1)} custom-call(bf16[32,48,512]{2,1,0:T(8,128)(2,1)} %all-to-all-done.1.received_ref, bf16[2,2048,2048]{2,1,0:T(8,128)(2,1)} %weights_ref.3), custom_call_target="tpu_custom_call" | custom-call | flops 6442450944 | tf_op jit(solution)/shard_map/first_beams/pallas_call | solution.py:337
  77.7 1.2 %all-to-all-done.received_ref = bf16[32,48,256]{2,1,0:T(8,128)(2,1)S(1)} async-done(((bf16[32,48,256]{2,1,0:T(8,128)(2,1)}), bf16[32,48,256]{2,1,0:T(8,128)(2,1)S(1)}, u32[]{:S(2)}, u32[]{:S(2)}) %all-to-all-start) | async-done | bytes 786464 | tf_op jit(solution)/shard_map/all_to_all | solution.py:335
  78.9 15.3 %last_beams.1 = bf16[32,24,128]{2,1,0:T(8,128)(2,1)} custom-call(bf16[32,48,256]{2,1,0:T(8,128)(2,1)S(1)} %all-to-all-done.received_ref, bf16[2,2048,2048]{2,1,0:T(8,128)(2,1)} %weights_ref.3, f32[24,2048]{1,0:T(8,128)S(1)} %first_beams.1.partial_ref, s32[16,128]{1,0:T(8,128)S(1)} %bitcast.5), custom_call_target="tpu_custom_call" | custom-call | flops 3221225472 | tf_op jit(solution)/shard_map/last_beams/pallas_call | solution.py:348
  94.2 6.2 %all-to-all-start.2 = ((bf16[32,24,128]{2,1,0:T(8,128)(2,1)}), bf16[32,24,128]{2,1,0:T(8,128)(2,1)S(1)}, u32[]{:S(2)}, u32[]{:S(2)}) async-start(bf16[32,24,128]{2,1,0:T(8,128)(2,1)} %last_beams.1), calls=%async_computation.2 | async-start | bytes 393216 | tf_op jit(solution)/shard_map/all_to_all | solution.py:367
  100.4 0.0 copy-start.11
  100.4 2.2 %copy-done.11 = f32[1024,1024]{1,0:T(8,128)S(1)} copy-done((f32[1024,1024]{1,0:T(8,128)S(1)}, f32[1024,1024]{1,0:T(8,128)}, u32[]{:S(2)}) %copy-start.11) | copy-done | bytes 4194328
  102.6 1.4 %copy-done.15 = bf16[768,1024]{1,0:T(8,128)(2,1)S(1)} copy-done((bf16[768,1024]{1,0:T(8,128)(2,1)S(1)}, bf16[768,1024]{1,0:T(8,128)(2,1)}, u32[]{:S(2)}) %copy-start.15) | copy-done | bytes 1572888
  104.0 3.4 %filter_rows.1 = (bf16[768,1024]{1,0:T(8,128)(2,1)S(1)}, bf16[768,1024]{1,0:T(8,128)(2,1)S(1)}) custom-call(bf16[768,1024]{1,0:T(8,128)(2,1)S(1)} %copy-done.15, f32[1024,1024]{1,0:T(8,128)S(1)} %copy-done.11), custom_call_target="tpu_custom_call" | custom-call | flops 3221225472 | tf_op jit(solution)/shard_map/filter_rows/pallas_call | solution.py:326
  107.5 1.3 %all-to-all-done.2 = bf16[32,24,128]{2,1,0:T(8,128)(2,1)S(1)} async-done(((bf16[32,24,128]{2,1,0:T(8,128)(2,1)}), bf16[32,24,128]{2,1,0:T(8,128)(2,1)S(1)}, u32[]{:S(2)}, u32[]{:S(2)}) %all-to-all-start.2) | async-done | bytes 196640 | tf_op jit(solution)/shard_map/all_to_all | solution.py:367
  108.7 1.3 %filter.1 = f32[64,1024]{1,0:T(8,128)} custom-call(bf16[768,128]{1,0:T(8,128)(2,1)S(1)} %bitcast.4, bf16[768,1024]{1,0:T(8,128)(2,1)S(1)} %get-tuple-element.15.high_ref, bf16[768,1024]{1,0:T(8,128)(2,1)S(1)} %get-tuple-element.16.low_ref), custom_call_target="tpu_custom_call" | custom-call | flops 402653184 | tf_op jit(solution)/shard_map/filter/pallas_call | solution.py:368
  (15 shorter events, 0.0 us)
Async XLA Ops:
  0.0 1.9 %copy-start.2 = (bf16[64,24576]{1,0:T(8,128)(2,1)S(1)}, bf16[64,24576]{1,0:T(8,128)(2,1)}, u32[]{:S(2)}) copy-start(bf16[64,24576]{1,0:T(8,128)(2,1)} %volts_ref.3) | copy-start | bytes 9437188
  1.9 0.8 copy-start.8
  2.6 0.9 copy-start.12
  3.6 0.7 copy-start.13
  14.1 2.7 %copy-start = (bf16[1536,2048]{1,0:T(8,128)(2,1)}, bf16[1536,2048]{1,0:T(8,128)(2,1)S(1)}, u32[]{:S(2)}) copy-start(bf16[1536,2048]{1,0:T(8,128)(2,1)S(1)} %get-tuple-element.11.table_ref) | copy-start | bytes 18874372
  16.8 1.2 %copy-start.5 = (bf16[32,48,512]{2,1,0:T(8,128)(2,1)}, bf16[32,48,512]{2,1,0:T(8,128)(2,1)S(1)}, u32[]{:S(2)}) copy-start(bf16[32,48,512]{2,1,0:T(8,128)(2,1)S(1)} %get-tuple-element.13) | copy-start | bytes 4718596
  18.0 0.9 copy-start.6
  18.9 1.1 %copy-start.14 = (bf16[768,1024]{1,0:T(8,128)(2,1)}, bf16[768,1024]{1,0:T(8,128)(2,1)S(1)}, u32[]{:S(2)}) copy-start(bf16[768,1024]{1,0:T(8,128)(2,1)S(1)} %get-tuple-element.14.pick_ref) | copy-start | bytes 4718596
  20.1 9.9 %copy-start.3 = (bf16[64,24576]{1,0:T(8,128)(2,1)S(1)}, bf16[64,24576]{1,0:T(8,128)(2,1)}, u32[]{:S(2)}) copy-start(bf16[64,24576]{1,0:T(8,128)(2,1)} %volts_ref.3) | copy-start | bytes 9437188
  20.1 36.4 %all-to-all-start.1 = ((bf16[32,48,512]{2,1,0:T(8,128)(2,1)}), bf16[32,48,512]{2,1,0:T(8,128)(2,1)}, u32[]{:S(2)}, u32[]{:S(2)}) async-start(bf16[32,48,512]{2,1,0:T(8,128)(2,1)} %copy-done.5), calls=%async_computation.1 | async-start | bytes 3145728 | tf_op jit(solution)/shard_map/all_to_all | solution.py:311
  30.0 19.9 %copy-start.7 = (f32[768,256]{1,0:T(8,128)S(1)}, f32[768,256]{1,0:T(8,128)}, u32[]{:S(2)}) copy-start(f32[768,256]{1,0:T(8,128)} %copy-done.6) | copy-start | bytes 2359300
  30.0 19.9 %copy-start.9 = (f32[4,2048]{1,0:T(4,128)S(1)}, f32[4,2048]{1,0:T(4,128)}, u32[]{:S(2)}) copy-start(f32[4,2048]{1,0:T(4,128)} %constant.2.clone.window_ref) | copy-start | bytes 98308
  30.1 19.8 %collective-permute-start = (bf16[64,6144]{1,0:T(8,128)(2,1)S(1)}, bf16[64,6144]{1,0:T(8,128)(2,1)S(1)}, u32[]{:S(2)}, u32[]{:S(2)}) collective-permute-start(bf16[64,6144]{1,0:T(8,128)(2,1)S(1)} %slice.3), channel_id=1, source_target_pairs={{0,32},{32,64},{64,96},{1,33},{33,65},{65,97},{2,34},{34,66},{66,9... | collective-permute-start | bytes 2359304 | tf_op jit(solution)/shard_map/ppermute | solution.py:290
  49.9 2.8 %copy-start.1 = (bf16[1536,2048]{1,0:T(8,128)(2,1)S(1)}, bf16[1536,2048]{1,0:T(8,128)(2,1)}, u32[]{:S(2)}) copy-start(bf16[1536,2048]{1,0:T(8,128)(2,1)} %copy-done) | copy-start | bytes 18874372
  55.6 0.9 copy-start.4
  56.5 22.4 %all-to-all-start = ((bf16[32,48,256]{2,1,0:T(8,128)(2,1)}), bf16[32,48,256]{2,1,0:T(8,128)(2,1)S(1)}, u32[]{:S(2)}, u32[]{:S(2)}) async-start(bf16[32,48,256]{2,1,0:T(8,128)(2,1)} %copy-done.4), calls=%async_computation | async-start | bytes 1572864 | tf_op jit(solution)/shard_map/all_to_all | solution.py:335
  64.6 14.2 %copy-start.10 = (s32[2048]{0:T(1024)S(1)}, s32[2048]{0:T(1024)}, u32[]{:S(2)}) copy-start(s32[2048]{0:T(1024)} %param.12) | copy-start | bytes 24580
  94.2 14.5 %all-to-all-start.2 = ((bf16[32,24,128]{2,1,0:T(8,128)(2,1)}), bf16[32,24,128]{2,1,0:T(8,128)(2,1)S(1)}, u32[]{:S(2)}, u32[]{:S(2)}) async-start(bf16[32,24,128]{2,1,0:T(8,128)(2,1)} %last_beams.1), calls=%async_computation.2 | async-start | bytes 393216 | tf_op jit(solution)/shard_map/all_to_all | solution.py:367
  100.4 2.2 %copy-start.11 = (f32[1024,1024]{1,0:T(8,128)S(1)}, f32[1024,1024]{1,0:T(8,128)}, u32[]{:S(2)}) copy-start(f32[1024,1024]{1,0:T(8,128)} %filter_ref.1) | copy-start | bytes 12582916
  102.6 1.4 %copy-start.15 = (bf16[768,1024]{1,0:T(8,128)(2,1)S(1)}, bf16[768,1024]{1,0:T(8,128)(2,1)}, u32[]{:S(2)}) copy-start(bf16[768,1024]{1,0:T(8,128)(2,1)} %copy-done.14) | copy-start | bytes 4718596
